TPU v7x, 32 devices: a whole 2x2x4 slice. The times are simulated.
32 devices in a mesh: sub: 8 (over z, y), slab: 4 (over x, core).
Axes of the slice: x: 2, y: 2, z: 4, core: 2. Of those that a mesh axis runs over, the one named last changes fastest.
Arguments:
- rhs: float32 [8, 64, 8, 512], P(None, 'sub', None, 'slab'), may hold values from -60 to 60, as said below
- perm: float32 [64, 8, 512], P('sub', None, 'slab'), may hold values from 0.1 to 10
- accum: float32 [64, 8, 512], P('sub', None, 'slab'), may hold values from 0.05 to 0.5
- counts: int32 [8], replicated, may hold values from 1 to 8, as said below
Outputs:
- solution: float32 [8, 64, 8, 512], P(None, 'sub', None, 'slab')
- residual: float32 [8, 64, 8, 512], P(None, 'sub', None, 'slab')
Inputs may be any that keep to these rules, and one draw needn't show every extreme that they name: `rhs`: pressure sources of the 8 systems; values on planes that are not live are never read. counts[i] live planes fill the first slots of subdomain i; some subdomain has 8.
All inputs are finite; a program needn't handle non-finite values.
Results may differ from a plain program's by a relative error of at most 0.00045.
Values sent between devices are 32-bit elements; how exact they have to be, the bound alone decides.
A program may use at most 64 MiB of HBM per device.

v0:
```python
import functools

import jax
import jax.numpy as jnp
from jax import lax
from jax.experimental import pallas as pl
from jax.experimental.pallas import tpu as pltpu
from jax.sharding import PartitionSpec as P

S = 8
ITERS = 4
DEG = 4


cheb_low = 0.05
cheb_high = 2.0


def with_halo(cells, sides, width):
    for axis, dim in sides:
        count = lax.axis_size(axis)
        ends = count - 1
        head = lax.slice_in_dim(cells, 0, width, axis=dim)
        tail = lax.slice_in_dim(cells, cells.shape[dim] - width, cells.shape[dim], axis=dim)
        cells = jnp.concatenate(
            [
                lax.ppermute(tail, axis, [(i, (i + 1) % count) for i in range(ends)]),
                cells,
                lax.ppermute(head, axis, [((i + 1) % count, i) for i in range(ends)]),
            ],
            axis=dim,
        )
    return cells


def neighbours(field, live, plane):
    first = field[:, 0]
    last = lax.dynamic_index_in_dim(field, live - 1, 1, keepdims=False)
    edges = with_halo(jnp.stack([first, last], axis=1), (("sub", 1),), 1)
    before = edges[:, 0:1]
    after = edges[:, 3:4]
    zero_plane = jnp.zeros_like(field[:, :1])
    up_inside = jnp.concatenate([field[:, 1:], zero_plane], axis=1)
    down_inside = jnp.concatenate([zero_plane, field[:, :-1]], axis=1)
    x_next = jnp.where(plane == live - 1, after, up_inside)
    x_prev = jnp.where(plane == 0, before, down_inside)
    zero_row = jnp.zeros_like(field[:, :, :1])
    y_next = jnp.concatenate([field[:, :, 1:], zero_row], axis=2)
    y_prev = jnp.concatenate([zero_row, field[:, :, :-1]], axis=2)
    padded = with_halo(field, (("slab", 3),), 1)
    z_next = padded[..., 2:]
    z_prev = padded[..., :-2]
    return (x_next, x_prev, y_next, y_prev, z_next, z_prev)


def product(left, right):
    return lax.dot_general(
        left.reshape(left.shape[0], -1),
        right.reshape(right.shape[0], -1),
        (((1,), (1,)), ((), ())),
        precision=lax.Precision.HIGHEST,
    )


def combine(coef, block):
    flat = jnp.dot(coef, block.reshape(block.shape[0], -1), precision=lax.Precision.HIGHEST)
    return flat.reshape(block.shape)


def lower_solve(factor, block):
    flat = jax.scipy.linalg.solve_triangular(factor, block.reshape(block.shape[0], -1), lower=True)
    return flat.reshape(block.shape)


def precondition(vector, operate, inv_diag):
    theta = 0.5 * (cheb_high + cheb_low)
    delta = 0.5 * (cheb_high - cheb_low)
    sigma = theta / delta
    remain = vector
    update = inv_diag * remain * (1.0 / theta)
    result = update
    rho = 1.0 / sigma
    for step in range(DEG - 1):
        remain = remain - operate(update)
        rho_next = 1.0 / (2.0 * sigma - rho)
        update = rho_next * rho * update + 2.0 * rho_next / delta * (inv_diag * remain)
        result = result + update
        rho = rho_next
    return result


def small_solve(coefs, lowers, lead):
    hess = jnp.zeros((ITERS * S, (ITERS + 1) * S), jnp.float32)
    for j in range(ITERS):
        for i in range(j + 1):
            hess = hess.at[j * S : (j + 1) * S, i * S : (i + 1) * S].set(coefs[j][i])
        hess = hess.at[j * S : (j + 1) * S, (j + 1) * S : (j + 2) * S].set(lowers[j])
    target = jnp.zeros((S, (ITERS + 1) * S), jnp.float32).at[:, :S].set(lead)
    normal = jnp.dot(hess, hess.T, precision=lax.Precision.HIGHEST)
    right = jnp.dot(hess, target.T, precision=lax.Precision.HIGHEST)
    factor = jnp.linalg.cholesky(normal)
    mix = jax.scipy.linalg.cho_solve((factor, True), right).T
    return (mix, hess, target)


def body(rhs, perm, accum, counts):
    live = counts[lax.axis_index("sub")]
    depth = rhs.shape[1]
    plane = lax.broadcasted_iota(jnp.int32, (1, depth, 1, 1), 1)
    mask = (plane < live).astype(jnp.float32)
    field_perm = perm[None]
    near = neighbours(field_perm, live, plane)
    conduct = []
    diag = accum[None]
    for other in near:
        weight = 2.0 * field_perm * other / (field_perm + other)
        conduct.append(weight)
        diag = diag + weight
    inv_diag = mask / diag

    def operate(field):
        beside = neighbours(field, live, plane)
        total = diag * field
        for weight, other in zip(conduct, beside):
            total = total - weight * other
        return mask * total

    start = rhs * mask
    lead = jnp.linalg.cholesky(lax.psum(product(start, start), ("sub", "slab")))
    basis = [lower_solve(lead, start)]
    coefs = []
    lowers = []
    for step in range(ITERS):
        direction = precondition(basis[step], operate, inv_diag)
        work = operate(direction)
        stacked, whole = lax.psum(
            (jnp.stack([product(work, basis[i]) for i in range(step + 1)]), product(work, work)),
            ("sub", "slab"),
        )
        found = [stacked[i] for i in range(step + 1)]
        block = whole
        for i in range(step + 1):
            work = work - combine(found[i], basis[i])
            block = block - jnp.dot(found[i], found[i].T, precision=lax.Precision.HIGHEST)
        lower = jnp.linalg.cholesky(block)
        basis.append(lower_solve(lower, work))
        coefs.append(found)
        lowers.append(lower)
    mix, hess, target = small_solve(coefs, lowers, lead)
    combo = combine(mix[:, :S], basis[0])
    for j in range(1, ITERS):
        combo = combo + combine(mix[:, j * S : (j + 1) * S], basis[j])
    solution = precondition(combo, operate, inv_diag)
    residual = start - operate(solution)
    return (solution, residual)

LANES = 128


def full(dims, left, right):
    return lax.dot_general(
        left,
        right,
        (dims, ((), ())),
        precision=lax.Precision.HIGHEST,
        preferred_element_type=jnp.float32,
    )


def chebyshev_steps():
    theta = 0.5 * (cheb_high + cheb_low)
    delta = 0.5 * (cheb_high - cheb_low)
    sigma = theta / delta
    rho = 1.0 / sigma
    steps = []
    for _ in range(DEG - 1):
        rho_next = 1.0 / (2.0 * sigma - rho)
        steps.append((rho_next * rho, 2.0 * rho_next / delta))
        rho = rho_next
    return 1.0 / theta, steps


def eliminate(mat, rows, jordan):
    row = lax.broadcasted_iota(jnp.int32, mat.shape, 0)
    for k in range(rows):
        column = jnp.broadcast_to(mat[:, k : k + 1], mat.shape)
        pivot = column[k : k + 1, :]
        line = mat[k : k + 1, :]
        if jordan:
            scaled = line / pivot
            mat = jnp.where(row == k, scaled, mat - column * scaled)
        else:
            root = lax.rsqrt(pivot)
            root = root * (1.5 - 0.5 * pivot * root * root)
            scaled = line * root
            mat = jnp.where(row == k, scaled, jnp.where(row > k, mat - column * root * scaled, mat))
    return mat


def kernel(
    dims,
    raw_ref, pick_ref, out_ref,
    ext, coef, big, near_lo, near_hi, d0, d1, rem, sol, start_own,
    part, got1, mid, got2, tmp, hess, normal,
    xs_send, xs_recv, halo_send, halo_recv, s1_send, s1_recv, s2_send, s2_recv,
):
    nsub, nslab, zl, yl_n, pack, nx = dims
    halo = DEG
    pad = halo + 1
    span = zl + 2 * halo
    per = yl_n + 1
    sub = lax.axis_index("sub")
    slab = lax.axis_index("slab")
    place = slab * nsub + sub
    total = nsub * nslab
    nxt = lax.rem(place + 1, total)
    prv = lax.rem(place + total - 1, total)

    def dev(g):
        return {"sub": lax.rem(g, nsub), "slab": g // nsub}

    barrier = pltpu.get_barrier_semaphore()
    for d in range(1, nslab):
        pl.semaphore_signal(
            barrier, inc=1, device_id={"slab": lax.rem(slab + d, nslab)}, device_id_type=pl.DeviceIdType.MESH
        )
    for d in range(1, nsub):
        pl.semaphore_signal(
            barrier, inc=1, device_id={"sub": lax.rem(sub + d, nsub)}, device_id_type=pl.DeviceIdType.MESH
        )
    for g in (nxt, prv):
        pl.semaphore_signal(barrier, inc=1, device_id=dev(g), device_id_type=pl.DeviceIdType.MESH)

    def remote(src, dst, send, recv, device):
        return pltpu.make_async_remote_copy(
            src_ref=src, dst_ref=dst, send_sem=send, recv_sem=recv,
            device_id=device, device_id_type=pl.DeviceIdType.MESH,
        )

    packed = full(((1,), (0,)), raw_ref[...], pick_ref[...])
    for k in range(zl * per):
        at = (pad * per + k) * LANES
        ext[:, at : at + LANES] = packed[k * 8 : k * 8 + 8, :]
    pl.semaphore_wait(barrier, nslab + nsub)

    edge = pad * per * LANES
    whole = zl * per * LANES
    up = remote(ext.at[:, whole : whole + edge], ext.at[:, 0:edge], xs_send.at[0], xs_recv.at[0], dev(nxt))
    down = remote(ext.at[:, edge : 2 * edge], ext.at[:, edge + whole : 2 * edge + whole], xs_send.at[1], xs_recv.at[1], dev(prv))
    up.start()
    down.start()

    lane = lax.broadcasted_iota(jnp.int32, (8, LANES), 1)
    row = lax.broadcasted_iota(jnp.int32, (8, LANES), 0)
    tile = yl_n * LANES
    own_lo, own_hi = halo * tile, (halo + zl) * tile

    for k in range(zl):
        a = (pad + k) * per * LANES
        start_own[:, k * tile : (k + 1) * tile] = ext[:, a : a + tile]
    part[...] = jnp.zeros_like(part)

    def reduce_begin(r, gram, width):
        part[r, :, 0:width] = gram
        got1[r, slab] = part[r]
        copies = []
        for d in range(1, nslab):
            peer = lax.rem(slab + d, nslab)
            c = remote(part.at[r], got1.at[r, slab], s1_send.at[r, d], s1_recv.at[r, slab], {"slab": peer})
            c.start()
            copies.append(c)
        return copies

    def reduce_end(r, copies):
        for d in range(1, nslab):
            peer = lax.rem(slab + d, nslab)
            remote(part.at[r], got1.at[r, peer], s1_send.at[r, d], s1_recv.at[r, peer], {"slab": peer}).wait_recv()
        acc = got1[r, 0]
        for i in range(1, nslab):
            acc = acc + got1[r, i]
        mid[r] = acc
        got2[r, sub] = acc
        for d in range(1, nsub):
            peer = lax.rem(sub + d, nsub)
            c = remote(mid.at[r], got2.at[r, sub], s2_send.at[r, d], s2_recv.at[r, sub], {"sub": peer})
            c.start()
            copies.append(c)
        for d in range(1, nsub):
            peer = lax.rem(sub + d, nsub)
            remote(mid.at[r], got2.at[r, peer], s2_send.at[r, d], s2_recv.at[r, peer], {"sub": peer}).wait_recv()
        acc = got2[r, 0]
        for i in range(1, nsub):
            acc = acc + got2[r, i]
        for c in copies:
            c.wait_send()
        return acc

    begun = reduce_begin(0, full(((1,), (1,)), start_own[...], start_own[...]), 8)

    up.wait()
    down.wait()
    low = jnp.where(place == 0, 0.0, 1.0).astype(jnp.float32)
    high = jnp.where(place == total - 1, 0.0, 1.0).astype(jnp.float32)
    for k in range(pad):
        a = (k * per + yl_n) * LANES
        ext[:, a : a + LANES] = ext[:, a : a + LANES] * low
        b = ((pad + zl + k) * per + yl_n) * LANES
        ext[:, b : b + LANES] = ext[:, b : b + LANES] * high
    along = lax.rem(lane, nx)

    def fill(e, _):
        def grab(t):
            return ext[:, pl.ds(pl.multiple_of(((e + 1 + t) * per + yl_n) * LANES, LANES), LANES)]

        here, after, before = grab(0), grab(1), grab(-1)
        swap_up = pltpu.roll(here, LANES - nx, 1)
        swap_down = pltpu.roll(here, nx, 1)
        x_up = jnp.where(along == nx - 1, 0.0, pltpu.roll(here, LANES - 1, 1))
        x_down = jnp.where(along == 0, 0.0, pltpu.roll(here, 1, 1))
        swap_up = jnp.where(lane >= LANES - nx, 0.0, swap_up)
        swap_down = jnp.where(lane < nx, 0.0, swap_down)

        def line(value, y):
            return jnp.broadcast_to(value[y : y + 1, :], (8, LANES))

        for y in range(yl_n):
            p = line(here, y)
            others = (
                line(x_up, y),
                line(x_down, y),
                line(here, y + 1) if y + 1 < yl_n else line(swap_up, 0),
                line(here, y - 1) if y > 0 else line(swap_down, yl_n - 1),
                line(after, y),
                line(before, y),
            )
            at = pl.ds(pl.multiple_of((e * yl_n + y) * LANES, LANES), LANES)
            diag = line(here, yl_n + y)
            for k, q in enumerate(others):
                both = p * q
                weight = jnp.where(both > 0.0, 2.0 * both / jnp.where(both > 0.0, p + q, 1.0), 0.0)
                coef[1 + k, :, at] = weight
                diag = diag + weight
            coef[0, :, at] = diag
            coef[7, :, at] = jnp.where(diag > 0.0, 1.0 / jnp.where(diag > 0.0, diag, 1.0), 0.0)
            big[0:8, at] = ext[:, pl.ds(pl.multiple_of(((e + 1) * per + y) * LANES, LANES), LANES)]
        return 0

    lax.fori_loop(0, span, fill, 0)

    first, steps = chebyshev_steps()

    def spot(e, y):
        return pl.ds(pl.multiple_of((e * yl_n + y) * LANES, LANES), LANES)

    def stencil(field, e):
        here = [field[:, spot(e, y)] for y in range(yl_n)]
        outs = []
        for y in range(yl_n):
            at = spot(e, y)
            f = here[y]
            y_up = here[y + 1] if y + 1 < yl_n else pltpu.roll(here[0], LANES - nx, 1)
            y_down = here[y - 1] if y > 0 else pltpu.roll(here[yl_n - 1], nx, 1)
            acc = coef[0, :, at] * f
            acc = acc - coef[1, :, at] * pltpu.roll(f, LANES - 1, 1)
            acc = acc - coef[2, :, at] * pltpu.roll(f, 1, 1)
            acc = acc - coef[3, :, at] * y_up
            acc = acc - coef[4, :, at] * y_down
            acc = acc - coef[5, :, at] * field[:, spot(e + 1, y)]
            acc = acc - coef[6, :, at] * field[:, spot(e - 1, y)]
            outs.append(acc)
        return here, outs

    def precondition_ref(load):
        def begin(e, _):
            for y in range(yl_n):
                at = spot(e, y)
                v = load(at)
                d = coef[7, :, at] * v * first
                rem[:, at] = v
                d0[:, at] = d
                sol[:, at] = d
            return 0

        lax.fori_loop(0, span, begin, 0)
        source, target = d0, d1
        for t, (keep, gain) in enumerate(steps):
            def one(e, _, source=source, target=target, keep=keep, gain=gain):
                here, outs = stencil(source, e)
                for y in range(yl_n):
                    at = spot(e, y)
                    r = rem[:, at] - outs[y]
                    rem[:, at] = r
                    d = keep * here[y] + gain * (coef[7, :, at] * r)
                    target[:, at] = d
                    sol[:, at] = sol[:, at] + d
                return 0

            lax.fori_loop(t + 1, span - t - 1, one, 0)
            source, target = target, source

    summed = reduce_end(0, begun)
    lead_mat = jnp.where(lane < 8, summed, 0.0) + jnp.where(lane == row + 64, 1.0, 0.0)
    done = eliminate(lead_mat, 8, False)
    lead_t = jnp.where(lane < 8, done, 0.0)
    inverse = pltpu.roll(done, 64, 1)
    big[8:16, :] = full(((1,), (0,)), inverse[:, 0:8], big[0:8, :])

    side = halo * tile
    for j in range(ITERS):
        r = j + 1
        base = 8 * (j + 1)
        precondition_ref(lambda at, base=base: big[base : base + 8, at])

        def apply(e, _):
            _, outs = stencil(sol, e)
            for y in range(yl_n):
                big[0:8, spot(e, y)] = outs[y]
            return 0

        lax.fori_loop(halo, halo + zl, apply, 0)
        moves = []
        if j < ITERS - 1:
            moves = [
                remote(big.at[0:8, own_hi - side : own_hi], near_lo.at[j], halo_send.at[j, 0], halo_recv.at[j, 0], dev(nxt)),
                remote(big.at[0:8, own_lo : own_lo + side], near_hi.at[j], halo_send.at[j, 1], halo_recv.at[j, 1], dev(prv)),
            ]
        width = 8 * (j + 2)
        gram = full(((1,), (1,)), big[0:8, own_lo:own_hi], big[0:width, own_lo:own_hi])
        begun = reduce_begin(r, gram, width)
        for m in moves:
            m.start()
        summed = reduce_end(r, begun)
        only = jnp.where(lane >= 8, summed, 0.0)
        tmp[...] = only + jnp.where(lane == row + 64, 1.0, 0.0)
        tmp[:, 0:8] = summed[:, 0:8] - full(((1,), (1,)), only, only)
        done = eliminate(tmp[...], 8, False)
        hess[8 * j : 8 * j + 8, :] = jnp.where(lane < base, pltpu.roll(summed, LANES - 8, 1), 0.0)
        hess[8 * j : 8 * j + 8, base : base + 8] = done.T[0:8, :]
        if j < ITERS - 1:
            for m in moves:
                m.wait()
            big[0:8, 0:own_lo] = near_lo[j]
            big[0:8, own_hi : own_hi + side] = near_hi[j]
            mixer = jnp.where(lane < 8, pltpu.roll(done, 64, 1), -done)
            big[base + 8 : base + 16, :] = full(((1,), (0,)), mixer[:, 0:width], big[0:width, :])

    rows = 8 * ITERS
    h = hess[...]
    normal[...] = jnp.zeros_like(normal)
    normal[:, 0:rows] = full(((1,), (1,)), h, h)
    normal[:, rows : rows + 8] = full(((1,), (0,)), h[:, 0:8], lead_t[:, 0:8])
    solved = eliminate(normal[...], rows, True)
    mix = solved.T[rows : rows + 8, :]
    big[0:8, :] = full(((1,), (0,)), mix, big[8 : 8 + rows, :])
    precondition_ref(lambda at: big[0:8, at])

    def finish(e, _):
        _, outs = stencil(sol, e)
        for y in range(yl_n):
            k = pl.multiple_of(((e - halo) * yl_n + y) * LANES, LANES)
            w = pl.multiple_of(((e - halo) * yl_n + y) * 8, 8)
            d0_at = pl.ds(w, 8)
            out_ref[0, d0_at, :] = sol[:, spot(e, y)]
            out_ref[1, d0_at, :] = start_own[:, pl.ds(k, LANES)] - outs[y]
        return 0

    lax.fori_loop(halo, halo + zl, finish, 0)
    for f in range(2):
        out_ref[f] = full(((1,), (1,)), out_ref[f], pick_ref[...])


def fast_body(rhs, perm, accum, counts):
    nsub, nslab = lax.axis_size("sub"), lax.axis_size("slab")
    s, depth, cy, zs = rhs.shape
    nx = depth * nsub
    pack = LANES // nx
    yl = cy // pack
    zl = zs // nsub
    span = zl + 2 * DEG
    pad = DEG + 1

    def turn(a):
        k = a.shape[0]
        a = a.reshape(k, depth, pack, yl, nsub, zl)
        return jnp.transpose(a, (4, 5, 3, 0, 2, 1)).reshape(nsub, zl, yl, k, pack * depth)

    fields = turn(rhs)
    pa = jnp.transpose(turn(jnp.stack([perm, accum])), (0, 1, 3, 2, 4)).reshape(nsub, zl, 1, 2 * yl, pack * depth)
    send = jnp.concatenate([fields, pa], axis=2)
    got = lax.all_to_all(send, "sub", 0, 0)
    raw = jnp.transpose(got, (1, 2, 3, 0, 4)).reshape(zl * (yl + 1) * s, LANES)

    before = jnp.cumsum(counts) - counts
    slot = jnp.arange(depth, dtype=jnp.int32)
    goal = jnp.where(slot[None] < counts[:, None], before[:, None] + slot[None], -1)
    half = jnp.arange(pack, dtype=jnp.int32)[None, :, None]
    goal = jnp.where(goal[:, None, :] >= 0, goal[:, None, :] + half * nx, -1).reshape(LANES, 1)
    pick = (goal == jnp.arange(LANES, dtype=jnp.int32)[None]).astype(jnp.float32)

    wide = span * yl * LANES
    f32 = jnp.float32
    rounds = ITERS + 1
    side = DEG * yl * LANES
    dma = pltpu.SemaphoreType.DMA
    out = pl.pallas_call(
        functools.partial(kernel, (nsub, nslab, zl, yl, pack, nx)),
        out_shape=jax.ShapeDtypeStruct((2, zl * yl * s, LANES), f32),
        in_specs=[pl.BlockSpec(memory_space=pltpu.VMEM)] * 2,
        out_specs=pl.BlockSpec(memory_space=pltpu.VMEM),
        scratch_shapes=[
            pltpu.VMEM((8, (zl + 2 * pad) * (yl + 1) * LANES), f32),
            pltpu.VMEM((8, 8, wide), f32),
            pltpu.VMEM((8 * (ITERS + 1), wide), f32),
            pltpu.VMEM((ITERS - 1, 8, side), f32),
            pltpu.VMEM((ITERS - 1, 8, side), f32),
            pltpu.VMEM((8, wide), f32),
            pltpu.VMEM((8, wide), f32),
            pltpu.VMEM((8, wide), f32),
            pltpu.VMEM((8, wide), f32),
            pltpu.VMEM((8, zl * yl * LANES), f32),
            pltpu.VMEM((rounds, 8, LANES), f32),
            pltpu.VMEM((rounds, nslab, 8, LANES), f32),
            pltpu.VMEM((rounds, 8, LANES), f32),
            pltpu.VMEM((rounds, nsub, 8, LANES), f32),
            pltpu.VMEM((8, LANES), f32),
            pltpu.VMEM((8 * ITERS, LANES), f32),
            pltpu.VMEM((8 * ITERS, LANES), f32),
            dma((2,)),
            dma((2,)),
            dma((ITERS - 1, 2)),
            dma((ITERS - 1, 2)),
            dma((rounds, nslab)),
            dma((rounds, nslab)),
            dma((rounds, nsub)),
            dma((rounds, nsub)),
        ],
        compiler_params=pltpu.CompilerParams(
            collective_id=0, has_side_effects=True, vmem_limit_bytes=48 * 1024 * 1024
        ),
    )(raw, pick)
    back = out.reshape(2, zl, yl, s, nsub, pack * depth)
    back = jnp.transpose(back, (4, 0, 1, 2, 3, 5))
    back = lax.all_to_all(back, "sub", 0, 0)
    back = back.reshape(nsub, 2, zl, yl, s, pack, depth)
    back = jnp.transpose(back, (1, 4, 6, 5, 3, 0, 2)).reshape(2, s, depth, cy, zs)
    return back[0], back[1]


def choose(rhs, perm, accum, counts):
    nsub = lax.axis_size("sub")
    s, depth, cy, zs = rhs.shape
    nx = depth * nsub
    fits = s == S == 8 and LANES % nx == 0 and zs % nsub == 0 and zs // nsub > DEG
    fits = fits and cy % max(LANES // nx, 1) == 0 and cy // max(LANES // nx, 1) == 4
    if fits:
        return fast_body(rhs, perm, accum, counts)
    return body(rhs, perm, accum, counts)


def solution(mesh):
    placed = (P(None, "sub", None, "slab"), P("sub", None, "slab"), P("sub", None, "slab"), P())
    return jax.shard_map(
        choose,
        mesh=mesh,
        in_specs=placed,
        out_specs=(P(None, "sub", None, "slab"), P(None, "sub", None, "slab")),
        check_vma=False,
    )
```

profile of v0, /device:TPU:0, one launch (start us, length us, event | category | flops | bytes accessed | tf_op | source)
XLA Modules:
  0.0 186.4 jit_solution(16392157573542384492)
XLA Ops:
  0.6 0.0 copy-start
  0.6 0.9 stack.9
  1.6 0.9 stack.10
  2.5 0.3 copy.21
  2.9 0.0 copy-done
  2.9 0.6 reshape.153
  3.5 1.2 copy.20
  4.7 0.3 fusion.2
  5.0 0.0 copy-start.1
  5.0 1.6 reshape.162
  6.7 7.3 %all-to-all-start = ((f32[8,1,10240]{2,1,0:T(1,128)}), f32[8,1,10240]{2,1,0:T(1,128)S(1)}, u32[]{:S(2)}, u32[]{:S(2)}) async-start(f32[8,1,10240]{2,1,0:T(1,128)} %reshape.162), calls=%async_computation | async-start | bytes 655360 | tf_op jit(solution)/shard_map/all_to_all | solution.py:490
  14.0 0.0 copy-done.1
  14.0 0.2 reduce-window.9
  14.2 0.1 add_select_fusion.1
  14.2 0.1 broadcast_compare_fusion
  14.3 0.1 add_select_fusion
  14.4 0.1 select_n.24
  14.5 0.1 fusion.pick_ref
  14.6 9.7 %all-to-all-done = f32[8,1,10240]{2,1,0:T(1,128)S(1)} async-done(((f32[8,1,10240]{2,1,0:T(1,128)}), f32[8,1,10240]{2,1,0:T(1,128)S(1)}, u32[]{:S(2)}, u32[]{:S(2)}) %all-to-all-start) | async-done | bytes 327712 | tf_op jit(solution)/shard_map/all_to_all | solution.py:490
  24.3 0.5 broadcast.68
  24.8 1.4 reduce
  26.2 0.9 reshape.163
  27.1 1.7 bitcast_bitcast_fusion.2
  28.8 3.3 %copy.14 = f32[16,5,8,8,16]{4,3,2,1,0:T(8,128)S(1)} copy(f32[16,5,8,8,16]{0,4,2,1,3:T(8,128)} %bitcast_bitcast_fusion.2) | data formatting | bytes 655360 | tf_op jit(solution)/shard_map/transpose | solution.py:491
  32.1 0.7 reshape.157.raw_ref
  32.8 102.7 %shard_map.59 = f32[2,512,128]{2,1,0:T(8,128)S(1)} custom-call(f32[640,128]{1,0:T(8,128)S(1)} %reshape.157.raw_ref, f32[128,128]{1,0:T(8,128)S(1)} %fusion.pick_ref), custom_call_target="tpu_custom_call" | custom-call | tf_op jit(solution)/shard_map/pallas_call | solution.py:505
  135.5 2.5 %reshape.160 = f32[2,16,4,8,8,16]{5,4,3,2,1,0:T(8,128)} reshape(f32[2,512,128]{2,1,0:T(8,128)S(1)} %shard_map.59) | data formatting | bytes 1048576 | tf_op jit(solution)/shard_map/reshape | solution.py:541
  138.0 5.9 %copy.15 = f32[2,16,4,8,8,16]{1,5,3,2,0,4:T(8,128)} copy(f32[2,16,4,8,8,16]{5,4,3,2,1,0:T(8,128)} %reshape.160) | data formatting | bytes 1048576 | tf_op jit(solution)/shard_map/reshape | solution.py:541
  143.9 4.7 %bitcast_bitcast_fusion.1 = f32[8,2,4,8,16,16]{5,4,3,2,1,0:T(8,128)} fusion(f32[2,16,4,8,8,16]{1,5,3,2,0,4:T(8,128)} %copy.15), kind=kLoop, calls=%fused_computation.14 | loop fusion | bytes 1048576
  148.6 3.7 %reshape.164 = f32[8,1,16384]{2,1,0:T(1,128)S(1)} reshape(f32[8,2,4,8,16,16]{5,4,3,2,1,0:T(8,128)} %bitcast_bitcast_fusion.1) | data formatting | bytes 1048576
  152.3 18.1 %all_to_all.10 = f32[8,1,16384]{2,1,0:T(1,128)S(1)} all-to-all(f32[8,1,16384]{2,1,0:T(1,128)S(1)} %reshape.164), channel_id=1, replica_groups=mesh['sub'=8,'slab'=4] {'sub'}, dimensions={0} | all-to-all | bytes 1048576 | tf_op jit(solution)/shard_map/all_to_all | solution.py:543
  170.4 1.9 %reduce.1 = f32[8,16384]{1,0:T(8,128)S(1)} reduce(f32[8,1,16384]{2,1,0:T(1,128)S(1)} %all_to_all.10, f32[]{:T(128)} %broadcast.68), dimensions={1}, to_apply=%all_to_all.7.reduce_sub_computation | reduce | bytes 1048580 | tf_op jit(solution)/shard_map/all_to_all | solution.py:543
  172.2 3.3 %reshape.165 = f32[8,2,4,8,16,16]{5,4,3,2,1,0:T(8,128)} reshape(f32[8,16384]{1,0:T(8,128)S(1)} %reduce.1) | data formatting | bytes 1048576
  175.6 2.5 %bitcast_bitcast_fusion = f32[2,8,8,2,4,8,16]{6,2,3,1,4,0,5:T(8,128)S(1)} fusion(f32[8,2,4,8,16,16]{5,4,3,2,1,0:T(8,128)} %reshape.165), kind=kLoop, calls=%fused_computation.13 | loop fusion | bytes 1048576 | tf_op jit(solution)/shard_map/transpose | solution.py:545
  178.1 1.8 fusion.1
  179.8 1.2 copy.17
  181.0 1.3 squeeze.7
  182.3 2.8 %copy.16 = f32[1,8,8,2,4,8,16]{6,5,4,3,2,1,0:T(8,128)S(1)} copy(f32[1,8,8,2,4,8,16]{6,2,3,1,4,0,5:T(8,128)} %get-tuple-element.3) | data formatting | bytes 524288 | tf_op jit(solution)/shard_map/slice | solution.py:546
  185.1 1.3 squeeze.6
  (4 shorter events, 0.1 us)
Async XLA Ops:
  0.6 2.3 %copy-start = (f32[8,8,8,128]{3,2,1,0:T(8,128)S(1)}, f32[8,8,8,128]{3,2,1,0:T(8,128)}, u32[]{:S(2)}) copy-start(f32[8,8,8,128]{3,2,1,0:T(8,128)} %param.4) | copy-start | bytes 786436
  5.0 9.0 %copy-start.1 = (s32[8]{0:T(128)S(1)}, s32[8]{0:T(128)}, u32[]{:S(2)}) copy-start(s32[8]{0:T(128)} %param.7) | copy-start | bytes 100
  6.7 17.6 %all-to-all-start = ((f32[8,1,10240]{2,1,0:T(1,128)}), f32[8,1,10240]{2,1,0:T(1,128)S(1)}, u32[]{:S(2)}, u32[]{:S(2)}) async-start(f32[8,1,10240]{2,1,0:T(1,128)} %reshape.162), calls=%async_computation | async-start | bytes 655360 | tf_op jit(solution)/shard_map/all_to_all | solution.py:490
where the time goes:
time: 187 us; the launch traced here: 186 us
  Pallas kernels  103 us (55%)
  local copies, waits for them, and re-layouts  43.7 us (23%)
  blocking collectives  18.1 us (10%)
  waiting for transfers between devices  9.68 us (5%)
  starting transfers between devices  7.31 us (4%)
  other arithmetic  4.14 us (2%)
    pallas_call x1, Pallas kernels, fast_body(): pl.pallas_call(functools.partial(kernel, (nsub, nslab, zl, yl, pack, nx))...  103 us
    all_to_all x1, blocking collectives, fast_body(): back = lax.all_to_all(back, 'sub', 0, 0)  18.1 us
    unnamed x9, local copies, waits for them, and re-layouts  14.2 us
    all_to_all x1, waiting for transfers between devices, fast_body(): got = lax.all_to_all(send, 'sub', 0, 0)  9.68 us
    reshape x2, local copies, waits for them, and re-layouts, fast_body(): back = out.reshape(2, zl, yl, s, nsub, pack * depth)  8.45 us
    all_to_all x1, starting transfers between devices, fast_body(): got = lax.all_to_all(send, 'sub', 0, 0)  7.31 us
    slice x3, local copies, waits for them, and re-layouts, fast_body(): return (back[0], back[1])  5.78 us
    transpose x2, local copies, waits for them, and re-layouts, fast_body(): raw = jnp.transpose(got, (1, 2, 3, 0, 4)).reshape(zl * (yl + 1) * s, LANES)  5.03 us
  transfers between devices with their start and end apart: 1, of which 1 were waited for; matrix products, arithmetic and copies ran while one was open for 0% of the time, Pallas kernels for 0%

commit v1 on v0

--- a/solution.py
+++ b/solution.py
@@ -199,10 +199,11 @@
 
 def kernel(
     dims,
-    raw_ref, pick_ref, out_ref,
+    rhs_ref, perm_ref, accum_ref, counts_ref, out0_ref, out1_ref,
+    pick_ref, raw_ref, out_ref, in_buf, in_got, out_buf, out_got,
     ext, coef, big, near_lo, near_hi, d0, d1, rem, sol, start_own,
     part, got1, mid, got2, tmp, hess, normal,
-    xs_send, xs_recv, halo_send, halo_recv, s1_send, s1_recv, s2_send, s2_recv,
+    in_send, in_recv, out_send, out_recv, xs_send, xs_recv, halo_send, halo_recv, s1_send, s1_recv, s2_send, s2_recv,
 ):
     nsub, nslab, zl, yl_n, pack, nx = dims
     halo = DEG
@@ -237,12 +238,67 @@
             device_id=device, device_id_type=pl.DeviceIdType.MESH,
         )
 
+    group = pack * (LANES // (pack * nsub))
+    wide_row = lax.broadcasted_iota(jnp.int32, (LANES, LANES), 0)
+    wide_lane = lax.broadcasted_iota(jnp.int32, (LANES, LANES), 1)
+    rank = lax.rem(wide_row, group) // pack
+    owner = wide_row // group
+    base_of = jnp.zeros_like(wide_row)
+    live_of = jnp.zeros_like(wide_row)
+    before = jnp.int32(0)
+    for i in range(nsub):
+        live = counts_ref[i]
+        base_of = jnp.where(owner == i, before, base_of)
+        live_of = jnp.where(owner == i, live, live_of)
+        before = before + live
+    goal = base_of + rank + lax.rem(wide_row, pack) * nx
+    pick_ref[...] = jnp.where((rank < live_of) & (goal == wide_lane), 1.0, 0.0).astype(jnp.float32)
+
+    for y in range(yl_n):
+        in_buf[y] = rhs_ref[pl.ds(y, LANES, stride=yl_n), :].T
+    pieces = [ref[pl.ds(y, group, stride=yl_n), :] for ref in (perm_ref, accum_ref) for y in range(yl_n)]
+    in_buf[yl_n] = jnp.concatenate(pieces, axis=0).T
+
+    pl.semaphore_wait(barrier, nslab + nsub)
+
+    def rows_of(i):
+        return pl.ds(pl.multiple_of(i * zl, 8), zl)
+
+    arrivals = []
+    for d in range(1, nsub):
+        peer = lax.rem(sub + d, nsub)
+        c = remote(in_buf.at[:, rows_of(peer), :], in_got.at[sub], in_send.at[d], in_recv.at[sub], {"sub": peer})
+        c.start()
+        arrivals.append(c)
+    in_got[sub] = in_buf[:, rows_of(sub), :]
+    for d in range(1, nsub):
+        peer = lax.rem(sub + d, nsub)
+        remote(in_buf.at[:, rows_of(peer), :], in_got.at[peer], in_send.at[d], in_recv.at[peer], {"sub": peer}).wait_recv()
+
+    strip = lax.broadcasted_iota(jnp.int32, (zl, LANES), 1) // group
+
+    def butterfly(items):
+        d = len(items) // 2
+        while d:
+            fresh = list(items)
+            for a in range(len(items)):
+                if a & d:
+                    continue
+                first_half = (strip & d) == 0
+                fresh[a] = jnp.where(first_half, items[a], pltpu.roll(items[a + d], group * d, 1))
+                fresh[a + d] = jnp.where(first_half, pltpu.roll(items[a], LANES - group * d, 1), items[a + d])
+            items = fresh
+            d //= 2
+        return items
+
+    for t in range(per):
+        for i, value in enumerate(butterfly([in_got[i, t] for i in range(nsub)])):
+            raw_ref[pl.ds(t * 8 + i, zl, stride=per * 8), :] = value
+
     packed = full(((1,), (0,)), raw_ref[...], pick_ref[...])
     for k in range(zl * per):
         at = (pad * per + k) * LANES
         ext[:, at : at + LANES] = packed[k * 8 : k * 8 + 8, :]
-    pl.semaphore_wait(barrier, nslab + nsub)
-
     edge = pad * per * LANES
     whole = zl * per * LANES
     up = remote(ext.at[:, whole : whole + edge], ext.at[:, 0:edge], xs_send.at[0], xs_recv.at[0], dev(nxt))
@@ -258,10 +314,34 @@
     for k in range(zl):
         a = (pad + k) * per * LANES
         start_own[:, k * tile : (k + 1) * tile] = ext[:, a : a + tile]
-    part[...] = jnp.zeros_like(part)
-
-    def reduce_begin(r, gram, width):
-        part[r, :, 0:width] = gram
+        big[0:8, (halo + k) * tile : (halo + k + 1) * tile] = ext[:, a : a + tile]
+
+    def products(blocks):
+        def add(k, accs):
+            accs = list(accs)
+            for h in range(2):
+                at = pl.ds(pl.multiple_of((2 * k + h) * LANES + own_lo, LANES), LANES)
+                w = big[0:8, at]
+                turned = [w] + [pltpu.roll(w, n, 0) for n in range(1, 8)]
+                for b in range(blocks):
+                    v = w if b == 0 else big[8 * b : 8 * b + 8, at]
+                    for n in range(8):
+                        accs[8 * b + n] = accs[8 * b + n] + v * turned[n]
+            return tuple(accs)
+
+        zero = jnp.zeros((8, LANES), jnp.float32)
+        accs = lax.fori_loop(0, zl * yl_n // 2, add, (zero,) * (8 * blocks))
+        out = zero
+        for b in range(blocks):
+            for n in range(8):
+                acc = accs[8 * b + n]
+                acc = pltpu.roll(acc, 8 - n, 0) if n else acc
+                line = jnp.sum(acc, axis=1, keepdims=True)
+                out = jnp.where(lane == 8 * b + lax.rem(row + n, 8), line, out)
+        return out
+
+    def reduce_begin(r, gram):
+        part[r] = gram
         got1[r, slab] = part[r]
         copies = []
         for d in range(1, nslab):
@@ -295,7 +375,7 @@
             c.wait_send()
         return acc
 
-    begun = reduce_begin(0, full(((1,), (1,)), start_own[...], start_own[...]), 8)
+    begun = reduce_begin(0, products(1))
 
     up.wait()
     down.wait()
@@ -350,6 +430,8 @@
     first, steps = chebyshev_steps()
 
     def spot(e, y):
+        if isinstance(e, int):
+            return pl.ds((e * yl_n + y) * LANES, LANES)
         return pl.ds(pl.multiple_of((e * yl_n + y) * LANES, LANES), LANES)
 
     def stencil(field, e):
@@ -370,32 +452,43 @@
             outs.append(acc)
         return here, outs
 
+    def sweep(lo, hi, work, chunk=4):
+        turns = (hi - lo) // chunk
+
+        def one(k, _):
+            work([lo + k * chunk + n for n in range(chunk)])
+            return 0
+
+        lax.fori_loop(0, turns, one, 0)
+        if lo + turns * chunk < hi:
+            work(list(range(lo + turns * chunk, hi)))
+
     def precondition_ref(load):
-        def begin(e, _):
-            for y in range(yl_n):
-                at = spot(e, y)
-                v = load(at)
-                d = coef[7, :, at] * v * first
-                rem[:, at] = v
-                d0[:, at] = d
-                sol[:, at] = d
-            return 0
-
-        lax.fori_loop(0, span, begin, 0)
+        def begin(es):
+            for e in es:
+                for y in range(yl_n):
+                    at = spot(e, y)
+                    v = load(at)
+                    d = coef[7, :, at] * v * first
+                    rem[:, at] = v
+                    d0[:, at] = d
+                    sol[:, at] = d
+
+        sweep(0, span, begin)
         source, target = d0, d1
         for t, (keep, gain) in enumerate(steps):
-            def one(e, _, source=source, target=target, keep=keep, gain=gain):
-                here, outs = stencil(source, e)
-                for y in range(yl_n):
-                    at = spot(e, y)
-                    r = rem[:, at] - outs[y]
-                    rem[:, at] = r
-                    d = keep * here[y] + gain * (coef[7, :, at] * r)
-                    target[:, at] = d
-                    sol[:, at] = sol[:, at] + d
-                return 0
-
-            lax.fori_loop(t + 1, span - t - 1, one, 0)
+            def one(es, source=source, target=target, keep=keep, gain=gain):
+                found = [stencil(source, e) for e in es]
+                for e, (here, outs) in zip(es, found):
+                    for y in range(yl_n):
+                        at = spot(e, y)
+                        r = rem[:, at] - outs[y]
+                        rem[:, at] = r
+                        d = keep * here[y] + gain * (coef[7, :, at] * r)
+                        target[:, at] = d
+                        sol[:, at] = sol[:, at] + d
+
+            sweep(t + 1, span - t - 1, one)
             source, target = target, source
 
     summed = reduce_end(0, begun)
@@ -411,13 +504,13 @@
         base = 8 * (j + 1)
         precondition_ref(lambda at, base=base: big[base : base + 8, at])
 
-        def apply(e, _):
-            _, outs = stencil(sol, e)
-            for y in range(yl_n):
-                big[0:8, spot(e, y)] = outs[y]
-            return 0
-
-        lax.fori_loop(halo, halo + zl, apply, 0)
+        def apply(es):
+            for e in es:
+                _, outs = stencil(sol, e)
+                for y in range(yl_n):
+                    big[0:8, spot(e, y)] = outs[y]
+
+        sweep(halo, halo + zl, apply)
         moves = []
         if j < ITERS - 1:
             moves = [
@@ -425,10 +518,9 @@
                 remote(big.at[0:8, own_lo : own_lo + side], near_hi.at[j], halo_send.at[j, 1], halo_recv.at[j, 1], dev(prv)),
             ]
         width = 8 * (j + 2)
-        gram = full(((1,), (1,)), big[0:8, own_lo:own_hi], big[0:width, own_lo:own_hi])
-        begun = reduce_begin(r, gram, width)
         for m in moves:
             m.start()
+        begun = reduce_begin(r, products(j + 2))
         summed = reduce_end(r, begun)
         only = jnp.where(lane >= 8, summed, 0.0)
         tmp[...] = only + jnp.where(lane == row + 64, 1.0, 0.0)
@@ -454,19 +546,37 @@
     big[0:8, :] = full(((1,), (0,)), mix, big[8 : 8 + rows, :])
     precondition_ref(lambda at: big[0:8, at])
 
-    def finish(e, _):
-        _, outs = stencil(sol, e)
+    def finish(es):
+        for e in es:
+            _, outs = stencil(sol, e)
+            for y in range(yl_n):
+                k = pl.multiple_of(((e - halo) * yl_n + y) * LANES, LANES)
+                w = pl.multiple_of(((e - halo) * yl_n + y) * 8, 8)
+                out_ref[0, pl.ds(w, 8), :] = sol[:, spot(e, y)]
+                out_ref[1, pl.ds(w, 8), :] = start_own[:, pl.ds(k, LANES)] - outs[y]
+
+    sweep(halo, halo + zl, finish)
+    for f in range(2):
+        raw_ref[0 : zl * yl_n * 8, :] = full(((1,), (1,)), out_ref[f], pick_ref[...])
         for y in range(yl_n):
-            k = pl.multiple_of(((e - halo) * yl_n + y) * LANES, LANES)
-            w = pl.multiple_of(((e - halo) * yl_n + y) * 8, 8)
-            d0_at = pl.ds(w, 8)
-            out_ref[0, d0_at, :] = sol[:, spot(e, y)]
-            out_ref[1, d0_at, :] = start_own[:, pl.ds(k, LANES)] - outs[y]
-        return 0
-
-    lax.fori_loop(halo, halo + zl, finish, 0)
-    for f in range(2):
-        out_ref[f] = full(((1,), (1,)), out_ref[f], pick_ref[...])
+            items = [raw_ref[pl.ds(y * 8 + i, zl, stride=yl_n * 8), :] for i in range(nsub)]
+            for i, value in enumerate(butterfly(items)):
+                out_buf[i, f * yl_n + y] = value
+    leaving = []
+    for d in range(1, nsub):
+        peer = lax.rem(sub + d, nsub)
+        c = remote(out_buf.at[peer], out_got.at[:, rows_of(sub), :], out_send.at[d], out_recv.at[sub], {"sub": peer})
+        c.start()
+        leaving.append(c)
+    out_got[:, rows_of(sub), :] = out_buf[sub]
+    for d in range(1, nsub):
+        peer = lax.rem(sub + d, nsub)
+        remote(out_buf.at[peer], out_got.at[:, rows_of(peer), :], out_send.at[d], out_recv.at[peer], {"sub": peer}).wait_recv()
+    for f, ref in enumerate((out0_ref, out1_ref)):
+        for y in range(yl_n):
+            ref[pl.ds(y, LANES, stride=yl_n), :] = out_got[f * yl_n + y].T
+    for c in arrivals + leaving:
+        c.wait_send()
 
 
 def fast_body(rhs, perm, accum, counts):
@@ -479,24 +589,6 @@
     span = zl + 2 * DEG
     pad = DEG + 1
 
-    def turn(a):
-        k = a.shape[0]
-        a = a.reshape(k, depth, pack, yl, nsub, zl)
-        return jnp.transpose(a, (4, 5, 3, 0, 2, 1)).reshape(nsub, zl, yl, k, pack * depth)
-
-    fields = turn(rhs)
-    pa = jnp.transpose(turn(jnp.stack([perm, accum])), (0, 1, 3, 2, 4)).reshape(nsub, zl, 1, 2 * yl, pack * depth)
-    send = jnp.concatenate([fields, pa], axis=2)
-    got = lax.all_to_all(send, "sub", 0, 0)
-    raw = jnp.transpose(got, (1, 2, 3, 0, 4)).reshape(zl * (yl + 1) * s, LANES)
-
-    before = jnp.cumsum(counts) - counts
-    slot = jnp.arange(depth, dtype=jnp.int32)
-    goal = jnp.where(slot[None] < counts[:, None], before[:, None] + slot[None], -1)
-    half = jnp.arange(pack, dtype=jnp.int32)[None, :, None]
-    goal = jnp.where(goal[:, None, :] >= 0, goal[:, None, :] + half * nx, -1).reshape(LANES, 1)
-    pick = (goal == jnp.arange(LANES, dtype=jnp.int32)[None]).astype(jnp.float32)
-
     wide = span * yl * LANES
     f32 = jnp.float32
     rounds = ITERS + 1
@@ -504,10 +596,17 @@
     dma = pltpu.SemaphoreType.DMA
     out = pl.pallas_call(
         functools.partial(kernel, (nsub, nslab, zl, yl, pack, nx)),
-        out_shape=jax.ShapeDtypeStruct((2, zl * yl * s, LANES), f32),
-        in_specs=[pl.BlockSpec(memory_space=pltpu.VMEM)] * 2,
-        out_specs=pl.BlockSpec(memory_space=pltpu.VMEM),
+        out_shape=[jax.ShapeDtypeStruct((s * depth * cy, zs), f32)] * 2,
+        in_specs=[pl.BlockSpec(memory_space=pltpu.VMEM)] * 3 + [pl.BlockSpec(memory_space=pltpu.SMEM)],
+        out_specs=[pl.BlockSpec(memory_space=pltpu.VMEM)] * 2,
         scratch_shapes=[
+            pltpu.VMEM((LANES, LANES), f32),
+            pltpu.VMEM((zl * (yl + 1) * s, LANES), f32),
+            pltpu.VMEM((2, zl * yl * s, LANES), f32),
+            pltpu.VMEM((yl + 1, zs, LANES), f32),
+            pltpu.VMEM((nsub, yl + 1, zl, LANES), f32),
+            pltpu.VMEM((nsub, 2 * yl, zl, LANES), f32),
+            pltpu.VMEM((2 * yl, zs, LANES), f32),
             pltpu.VMEM((8, (zl + 2 * pad) * (yl + 1) * LANES), f32),
             pltpu.VMEM((8, 8, wide), f32),
             pltpu.VMEM((8 * (ITERS + 1), wide), f32),
@@ -525,6 +624,10 @@
             pltpu.VMEM((8, LANES), f32),
             pltpu.VMEM((8 * ITERS, LANES), f32),
             pltpu.VMEM((8 * ITERS, LANES), f32),
+            dma((nsub,)),
+            dma((nsub,)),
+            dma((nsub,)),
+            dma((nsub,)),
             dma((2,)),
             dma((2,)),
             dma((ITERS - 1, 2)),
@@ -537,20 +640,15 @@
         compiler_params=pltpu.CompilerParams(
             collective_id=0, has_side_effects=True, vmem_limit_bytes=48 * 1024 * 1024
         ),
-    )(raw, pick)
-    back = out.reshape(2, zl, yl, s, nsub, pack * depth)
-    back = jnp.transpose(back, (4, 0, 1, 2, 3, 5))
-    back = lax.all_to_all(back, "sub", 0, 0)
-    back = back.reshape(nsub, 2, zl, yl, s, pack, depth)
-    back = jnp.transpose(back, (1, 4, 6, 5, 3, 0, 2)).reshape(2, s, depth, cy, zs)
-    return back[0], back[1]
+    )(rhs.reshape(-1, zs), perm.reshape(-1, zs), accum.reshape(-1, zs), counts)
+    return out[0].reshape(rhs.shape), out[1].reshape(rhs.shape)
 
 
 def choose(rhs, perm, accum, counts):
     nsub = lax.axis_size("sub")
     s, depth, cy, zs = rhs.shape
     nx = depth * nsub
-    fits = s == S == 8 and LANES % nx == 0 and zs % nsub == 0 and zs // nsub > DEG
+    fits = s == S == nsub == 8 and zs == LANES and zs // nsub % 8 == 0 and LANES % nx == 0 and zs % nsub == 0 and zs // nsub > DEG
     fits = fits and cy % max(LANES // nx, 1) == 0 and cy // max(LANES // nx, 1) == 4
     if fits:
         return fast_body(rhs, perm, accum, counts)

time: 187 us -> 105 us (0.56)
  local copies, waits for them, and re-layouts: 43.7 us -> 4.52 us
  blocking collectives: 18.1 us -> 0 us
  waiting for transfers between devices: 9.68 us -> 0 us
  starting transfers between devices: 7.31 us -> 0 us
  other arithmetic: 4.14 us -> 0 us
  Pallas kernels: 103 us -> 99 us
    all_to_all x1 -> x0, blocking collectives: 18.1 us -> none  [fast_body(): back = lax.all_to_all(back, 'sub', 0, 0)]
    reshape x4 -> x0, local copies, waits for them, and re-layouts: 9.72 us -> none  [the longest x2 8.45 us: fast_body(): back = out.reshape(2, zl, yl, s, nsub, pack * depth)]
    all_to_all x1 -> x0, waiting for transfers between devices: 9.68 us -> none  [fast_body(): got = lax.all_to_all(send, 'sub', 0, 0)]
    unnamed x9 -> x10, local copies, waits for them, and re-layouts: 14.2 us -> 4.52 us
    transpose x6 -> x0, local copies, waits for them, and re-layouts: 9.09 us -> none  [the longest x2 5.03 us: fast_body(): raw = jnp.transpose(got, (1, 2, 3, 0, 4)).reshape(zl * (yl + 1) * s, LANES)]
    all_to_all x1 -> x0, starting transfers between devices: 7.31 us -> none  [fast_body(): got = lax.all_to_all(send, 'sub', 0, 0)]
    slice x3 -> x0, local copies, waits for them, and re-layouts: 5.78 us -> none  [fast_body(): return (back[0], back[1])]
    pallas_call x1, Pallas kernels: 103 us -> 99 us  [fast_body(): pl.pallas_call(functools.partial(kernel, (nsub, nslab, zl, yl, pack, nx))...]
  transfers between devices with their start and end apart: 1 -> 0, of which waited for: 1 -> 0; matrix products, arithmetic and copies ran while one was open for 0% -> 0% of each run, Pallas kernels for 0% -> 0%
where the time goes in v1:
time: 105 us; the launch traced here: 104 us
  Pallas kernels  99 us (94%)
  local copies, waits for them, and re-layouts  4.52 us (4%)
    pallas_call x1, Pallas kernels, fast_body(): pl.pallas_call(functools.partial(kernel, (nsub, nslab, zl, yl, pack, nx))...  99 us
    unnamed x10, local copies, waits for them, and re-layouts  4.52 us

profile of v1, /device:TPU:0, one launch (start us, length us, event | category | flops | bytes accessed | tf_op | source)
XLA Modules:
  0.0 104.1 jit_solution(15179617547199476884)
XLA Ops:
  0.6 0.0 copy-start.3
  0.6 0.6 copy-done.3
  1.3 0.0 copy-start
  1.3 0.9 copy-done
  2.2 0.0 copy-start.1
  2.2 0.8 copy-done.1
  3.0 0.0 copy-start.2
  3.0 0.8 copy-done.2
  3.8 99.0 %shard_map.59 = (f32[512,128]{1,0:T(8,128)S(1)}, f32[512,128]{1,0:T(8,128)S(1)}) custom-call(f32[512,128]{1,0:T(8,128)S(1)} %bitcast.5, f32[64,128]{1,0:T(8,128)S(1)} %bitcast.8, f32[64,128]{1,0:T(8,128)S(1)} %bitcast.9, s32[8]{0:T(128)S(1)} %copy-done.3), custom_call_target="tpu_custom_call" | custom-call | tf_op jit(solution)/shard_map/pallas_call | solution.py:597
  102.7 0.7 copy.8
  103.4 0.7 copy.9
Async XLA Ops:
  0.6 0.7 copy-start.3
  1.3 0.9 copy-start
  2.2 0.8 copy-start.1
  3.0 0.8 copy-start.2
